TPU v7x, 32 devices: a whole 2x2x4 slice. The times are simulated.
32 devices in a mesh: tile: 16 (over z, y, x), lev: 2 (over core).
Axes of the slice: x: 2, y: 2, z: 4, core: 2. Of those that a mesh axis runs over, the one named last changes fastest.
Arguments:
- increments: bfloat16 [136, 256, 1024], P('lev', 'tile'), may hold values from -30 to 30
- projection: bfloat16 [80, 136], replicated, may hold values from -0.5 to 0.5
- helmholtz: float32 [80], P('lev'), may hold values from 0.05 to 4
Outputs:
- solution: float32 [80, 256, 1024], P('lev', 'tile')
- residual: float32 [80, 256, 1024], P('lev', 'tile')
All inputs are finite; a program needn't handle non-finite values.
Results may differ from a plain program's by a relative error of at most 0.00075.
Values may be sent and summed in bfloat16 or wider, within the bound.
A program may use at most 192 MiB of HBM per device.

v0:
```python
import functools

import jax
import jax.numpy as jnp
from jax import lax
from jax.experimental import pallas as pl
from jax.experimental.pallas import tpu as pltpu
from jax.sharding import PartitionSpec as P

S = 4
HALO = 2 * S
POWER = 13
UNROLL = 1
SUB = 8
LANE = 128
MESH = pl.DeviceIdType.MESH
f32 = jnp.float32
bf16 = jnp.bfloat16


def stage_groups(count):
    groups = []
    while count > 1:
        size = 4 if count % 4 == 0 else (2 if count % 2 == 0 else count)
        groups.append(size)
        count //= size
    return groups


def encode(value, scale):
    a = value * scale
    a4 = (a * a) * (a * a)
    return ((a4 * a4) * (a4 * a)).astype(bf16)


def decode(code, scale):
    code = code.astype(f32)
    size = jnp.exp(jnp.log(jnp.maximum(jnp.abs(code), 2.0 ** -126)) * (1.0 / POWER)) * (1.0 / scale)
    return jnp.where(code > 0.0, size, jnp.where(code < 0.0, -size, 0.0))


def spread(tile, times):
    return jnp.concatenate([tile] * times, axis=1)


def add(left, right):
    if left is None:
        return right
    if right is None:
        return left
    return left + right


def scaled(factor, vector):
    return [None if entry is None else factor * entry for entry in vector]


def added(left, right):
    return [add(a, b) for a, b in zip(left, right)]


def minus(left, right):
    result = []
    for a, b in zip(left, right):
        if b is None:
            result.append(a)
        elif a is None:
            result.append(-b)
        else:
            result.append(a - b)
    return result


def form(gram, left, right):
    total = None
    for a, left_entry in enumerate(left):
        if left_entry is None:
            continue
        inner = None
        for b, right_entry in enumerate(right):
            if right_entry is not None:
                inner = add(inner, gram(a, b) * right_entry)
        total = add(total, left_entry * inner)
    return total


def recurrence(gram, shift, p_coef, r_coef):
    x_coef = [None] * len(p_coef)
    squares = form(gram, r_coef, r_coef)
    for step in range(S):
        moved = minus(p_coef, shift(p_coef))
        alpha = squares / form(gram, p_coef, moved)
        x_coef = added(x_coef, scaled(alpha, p_coef))
        r_coef = minus(r_coef, scaled(alpha, moved))
        fresh = form(gram, r_coef, r_coef)
        p_coef = added(r_coef, scaled(fresh / squares, p_coef))
        squares = fresh
    return x_coef, r_coef, p_coef


def kernel(tiles, levs, groups, rows, modes, cells, levels, inc_ref, proj_ref, helm_ref, sol_ref, res_ref,
           x_all, wide, fields, dirs, res0, extra, total, out_buf, in_buf, weights, sums, coefs, grams,
           local_sems, swap_send, swap_recv, halo_send, halo_recv, gram_send, gram_recv):
    tile = lax.axis_index("tile")
    lev = lax.axis_index("lev")
    part = inc_ref.shape[0]
    across = cells // LANE
    parts_m = modes // SUB
    barrier = pltpu.get_barrier_semaphore()

    stage_peers = []
    stride = 1
    for size in groups:
        digit = lax.rem(lax.div(tile, stride), size)
        base = tile - digit * stride
        peers = []
        for j in range(1, size):
            peers.append(base + lax.rem(digit + j, size) * stride)
        stage_peers.append((digit, peers))
        stride *= size

    count = 0
    for j in range(1, levs):
        pl.semaphore_signal(barrier, 1, device_id=(tile, lax.rem(lev + j, levs)), device_id_type=MESH)
        count += 1
    for peer in (lax.rem(tile + 1, tiles), lax.rem(tile + tiles - 1, tiles)):
        pl.semaphore_signal(barrier, 1, device_id=(peer, lev), device_id_type=MESH)
        count += 1
    for digit, peers in stage_peers:
        for peer in peers:
            pl.semaphore_signal(barrier, 1, device_id=(peer, lev), device_id_type=MESH)
            count += 1

    local = pltpu.make_async_copy(inc_ref, x_all.at[0], local_sems.at[0])
    local.start()

    proj = proj_ref[...].astype(f32)
    own = proj[0:modes]
    for j in range(1, levs):
        own = jnp.where(lev == j, proj[j * modes:(j + 1) * modes], own)
    own_levels = levels // levs
    groups_l = [own[:, j * own_levels:(j + 1) * own_levels] for j in range(levs)]
    depth = part
    col_e = lax.broadcasted_iota(jnp.int32, (own_levels, depth), 1)
    row_e = lax.broadcasted_iota(jnp.int32, (own_levels, depth), 0) * rows
    onehot = jnp.where((col_e >= row_e) & (col_e < row_e + rows), 1.0, 0.0).astype(bf16)
    col_w = lax.rem(lax.broadcasted_iota(jnp.int32, (2 * modes, depth), 1), rows)
    second = jnp.where(lax.broadcasted_iota(jnp.int32, (2 * modes, depth), 0) >= modes, 1, 0)
    pick = col_w - second

    def widen(position):
        chosen = groups_l[position]
        for j in range(1, levs):
            chosen = jnp.where(lev == j, groups_l[(j + position) % levs], chosen)
        twice = jnp.concatenate([chosen, chosen], axis=0).astype(bf16)
        repeated = jnp.dot(twice, onehot, preferred_element_type=f32)
        for pair in range(rows // 2):
            wide[position, pair * 2 * modes:(pair + 1) * 2 * modes, :] = jnp.where(
                pick == 2 * pair, repeated, 0.0).astype(bf16)

    widen(0)
    pl.semaphore_wait(barrier, count)
    swaps = []
    for j in range(1, levs):
        copy = pltpu.make_async_remote_copy(
            src_ref=inc_ref, dst_ref=x_all.at[levs - j], send_sem=swap_send.at[j - 1],
            recv_sem=swap_recv.at[j - 1], device_id=(tile, lax.rem(lev + j, levs)), device_id_type=MESH)
        copy.start()
        swaps.append(copy)

    diag = lax.broadcasted_iota(jnp.int32, (modes, modes), 0) == lax.broadcasted_iota(jnp.int32, (modes, modes), 1)
    helm = jnp.sum(jnp.where(diag, jnp.broadcast_to(helm_ref[...], (modes, modes)), 0.0), axis=1, keepdims=True)
    weight = jnp.broadcast_to(1.0 / (4.0 + helm), (modes, LANE))
    weights[0] = weight
    weights[1] = jnp.where(tile > 0, weight, 0.0)
    weights[2] = jnp.where(tile < tiles - 1, weight, 0.0)
    sums[...] = jnp.zeros_like(sums)

    base_row = HALO
    field = fields.at[0]
    block = 2 * LANE if cells % (2 * LANE) == 0 else LANE

    def project_part(position):
        def project(index, carry):
            cols = pl.ds(pl.multiple_of(index * block, block), block)
            got = jnp.dot(wide[position], x_all[position, :, cols], preferred_element_type=f32)
            got = got.reshape(rows, modes, block)
            if position:
                got = field[base_row:base_row + rows, :, cols] + got
            field[base_row:base_row + rows, :, cols] = got
            return carry

        lax.fori_loop(0, cells // block, project, 0)

    local.wait()
    project_part(0)
    for j in range(1, levs):
        widen(j)
    for j in range(1, levs):
        swaps[j - 1].wait()
    for j in range(1, levs):
        project_part(j)

    slots = HALO // 2
    scale = 2.0 ** 9.7 / (0.5 * 30.0 * levels)

    def own_pair(side, pair):
        first = 2 * pair if side == 0 else rows - 2 - 2 * pair
        return field[base_row + first:base_row + first + 2].reshape(2 * modes, cells)

    def halo_copy(side, slot):
        peer = lax.rem(tile + tiles - 1, tiles) if side == 0 else lax.rem(tile + 1, tiles)
        return pltpu.make_async_remote_copy(
            src_ref=out_buf.at[side, slot], dst_ref=in_buf.at[side, slot], send_sem=halo_send.at[side, slot],
            recv_sem=halo_recv.at[side, slot], device_id=(peer, lev), device_id_type=MESH)

    for slot in range(slots):
        for side in range(2):
            out_buf[side, slot] = encode(own_pair(side, slot), scale)

        @pl.when(tile > 0)
        def _(slot=slot):
            halo_copy(0, slot).start()

        @pl.when(tile < tiles - 1)
        def _(slot=slot):
            halo_copy(1, slot).start()

    has = {0: tile < tiles - 1, 1: tile > 0}

    def take(side, pair):
        first = base_row + rows + 2 * pair if side == 0 else base_row - 2 - 2 * pair

        @pl.when(has[side])
        def _():
            halo_copy(side, pair).wait_recv()
            field[first:first + 2] = decode(in_buf[side, pair], scale).reshape(2, modes, cells)

        @pl.when(jnp.logical_not(has[side]))
        def _():
            field[first:first + 2] = jnp.zeros((2, modes, cells), f32)

    lane = lax.broadcasted_iota(jnp.int32, (SUB, LANE), 1)
    first_lane = lane == 0
    last_lane = lane == LANE - 1
    nothing = jnp.zeros((SUB, LANE), f32)

    def beside(tile_row):
        pieces = [tile_row[:, j * LANE:(j + 1) * LANE] for j in range(across)]
        right = [pltpu.roll(piece, 1, 1) for piece in pieces]
        left = [pltpu.roll(piece, LANE - 1, 1) for piece in pieces]
        result = []
        for j in range(across):
            low = jnp.where(first_lane, right[j - 1] if j else nothing, right[j])
            high = jnp.where(last_lane, left[j + 1] if j + 1 < across else nothing, left[j])
            result.append(low + high)
        return jnp.concatenate(result, axis=1)

    def fold(product):
        pieces = [product[:, j * LANE:(j + 1) * LANE] for j in range(across)]
        while len(pieces) > 1:
            pieces = [pieces[i] + pieces[i + 1] if i + 1 < len(pieces) else pieces[i] for i in range(0, len(pieces), 2)]
        return pieces[0]

    def over_rows(low, high, body):
        if high <= low:
            return
        if high - low == 1:
            body(low)
            return

        def step(index, carry):
            body(index)
            return carry

        lax.fori_loop(low, high, step, 0, unroll=UNROLL if (high - low) % UNROLL == 0 else 1)

    def apply(src, src_off, dst, dst_off, low, high, pairs=(), which=0):
        def body(row):
            for m in range(parts_m):
                at = slice(m * SUB, (m + 1) * SUB)
                here = src[row + src_off, at, :]
                around = src[row + src_off - 1, at, :] + src[row + src_off + 1, at, :] + beside(here)
                fresh = spread(weights[which, at, :], across) * around
                dst[row + dst_off, at, :] = fresh
                cache = {"src": here, "dst": fresh}
                for slot, left, right in pairs:
                    values = []
                    for operand in (left, right):
                        if isinstance(operand, str):
                            values.append(cache[operand])
                        else:
                            ref, off = operand
                            values.append(ref[row + off, at, :])
                    sums[slot, at, :] = sums[slot, at, :] + fold(values[0] * values[1])

        over_rows(low, high, body)

    def apply_all(src, src_off, dst, dst_off, wide_by, pairs):
        apply(src, src_off, dst, dst_off, -wide_by, 0, which=1)
        apply(src, src_off, dst, dst_off, 0, rows, pairs)
        apply(src, src_off, dst, dst_off, rows, rows + wide_by, which=2)

    def power_pairs(power):
        found = [(2 * power - 1, "src", "dst"), (2 * power, "dst", "dst")]
        if power == 1:
            found.append((0, "src", "src"))
        return found

    for power in range(1, S + 1):
        apply(fields.at[power - 1], HALO, fields.at[power], HALO, power, rows - power, power_pairs(power))
    for pair in range(S // 2):
        for side in range(2):
            take(side, pair)
    for power in range(1, S + 1):
        src, dst = fields.at[power - 1], fields.at[power]
        found = power_pairs(power)
        apply(src, HALO, dst, HALO, power - S, 0, which=1)
        apply(src, HALO, dst, HALO, 0, power, found)
        apply(src, HALO, dst, HALO, rows - power, rows, found)
        apply(src, HALO, dst, HALO, rows, rows + S - power, which=2)

    def packed(number):
        lanes = lax.broadcasted_iota(jnp.int32, (modes, LANE), 1)
        table = jnp.zeros((modes, LANE), f32)
        for slot in range(number):
            table = jnp.where(lanes == slot, jnp.sum(sums[slot], axis=1, keepdims=True), table)
        return table

    def gram_copies(block_index, stage):
        digit, peers = stage_peers[stage]
        size = groups[stage]
        sends = []
        for j in range(1, size):
            sends.append(pltpu.make_async_remote_copy(
                src_ref=grams.at[block_index, stage, digit], dst_ref=grams.at[block_index, stage, digit],
                send_sem=gram_send.at[block_index, stage, j - 1], recv_sem=gram_recv.at[block_index, stage, digit],
                device_id=(peers[j - 1], lev), device_id_type=MESH))
        return sends

    def gram_start(block_index, stage, table):
        grams[block_index, stage, stage_peers[stage][0]] = table
        for copy in gram_copies(block_index, stage):
            copy.start()

    def gram_finish(block_index, stage):
        digit, peers = stage_peers[stage]
        size = groups[stage]
        for copy in gram_copies(block_index, stage):
            copy.wait_send()
        for j in range(1, size):
            sender = lax.rem(digit + j, size)
            pltpu.make_async_remote_copy(
                src_ref=grams.at[block_index, stage, sender], dst_ref=grams.at[block_index, stage, sender],
                send_sem=gram_send.at[block_index, stage, j - 1], recv_sem=gram_recv.at[block_index, stage, sender],
                device_id=(peers[j - 1], lev), device_id_type=MESH).wait_recv()
        table = grams[block_index, stage, 0]
        for j in range(1, size):
            table = table + grams[block_index, stage, j]
        return table

    def column(table, slot):
        return jnp.broadcast_to(table[:, slot:slot + 1], (modes, LANE))

    def finish_all(block_index, table):
        for stage in range(len(groups)):
            if stage:
                gram_start(block_index, stage, table)
            table = gram_finish(block_index, stage)
        return table

    table = packed(2 * S + 1)
    gram_start(0, 0, table)

    for pair in range(S // 2, HALO // 2):
        for side in range(2):
            take(side, pair)
    for power in range(1, S + 1):
        src, dst = fields.at[power - 1], fields.at[power]
        apply(src, HALO, dst, HALO, power - HALO, power - S, which=1)
        apply(src, HALO, dst, HALO, rows + S - power, rows + HALO - power, which=2)
    sums[...] = jnp.zeros_like(sums)

    table = finish_all(0, table)
    moments = [column(table, slot) for slot in range(2 * S + 1)]
    one = jnp.ones((modes, LANE), f32)
    start = [one] + [None] * S
    x_coef, r_coef, p_coef = recurrence(
        lambda a, b: moments[a + b], lambda vector: [None] + vector[:-1], start, start)

    def keep(lists):
        position, kept = 0, []
        for entries in lists:
            places = []
            for index, entry in enumerate(entries):
                if entry is not None:
                    coefs[position] = entry
                    places.append((index, position))
                    position += 1
            kept.append(places)
        return kept

    def combined(places, values, at):
        result = None
        for index, position in places:
            result = add(result, spread(coefs[position, at, :], across) * values[index])
        return result

    x_at, r_at, p_at = keep([x_coef, r_coef, p_coef])

    def mix(low, high, inside):
        def body(row):
            for m in range(parts_m):
                at = slice(m * SUB, (m + 1) * SUB)
                values = [fields[power, row + HALO, at, :] for power in range(S + 1)]
                if inside:
                    total[row, at, :] = combined(x_at, values, at)
                res0[row + S, at, :] = combined(r_at, values, at)
                dirs[row + S, at, :] = combined(p_at, values, at)

        over_rows(low, high, body)

    mix(-S, 0, False)
    mix(0, rows, True)
    mix(rows, rows + S, False)

    d_refs = [(dirs, S)] + [(fields.at[power], HALO) for power in range(1, S + 1)]
    r_refs = [(res0, S), (fields.at[0], HALO)] + [(extra.at[power], S) for power in range(S - 2)]
    md, mr, cross = 0, 2 * S + 1, 4 * S
    for power in range(1, S + 1):
        found = [(md + 2 * power - 1, "src", "dst"), (md + 2 * power, "dst", "dst")]
        if power == 1:
            found.append((md, "src", "src"))
        apply_all(*d_refs[power - 1], *d_refs[power], S - power, found)
    for power in range(1, S):
        found = [(mr + 2 * power - 1, "src", "dst"), (mr + 2 * power, "dst", "dst"),
                 (cross + 2 * power, d_refs[power], "dst"), (cross + 2 * power + 1, d_refs[power + 1], "dst")]
        if power == 1:
            found += [(mr, "src", "src"), (cross, d_refs[0], "src"), (cross + 1, d_refs[1], "src")]
        apply_all(*r_refs[power - 1], *r_refs[power], S - 1 - power, found)

    number = 6 * S
    table = packed(number)
    gram_start(1, 0, table)
    table = finish_all(1, table)
    moments = [column(table, slot) for slot in range(number)]

    def gram(a, b):
        if a > S and b > S:
            return moments[mr + a + b - 2 * S - 2]
        if a > S or b > S:
            return moments[cross + a + b - S - 1]
        return moments[md + a + b]

    def shift(vector):
        return [None] + vector[:S] + [None] + vector[S + 1:2 * S]

    x_coef, r_coef, p_coef = recurrence(
        gram, shift, [one] + [None] * (2 * S), [None] * (S + 1) + [one] + [None] * (S - 1))
    x_at, r_at = keep([x_coef, r_coef])

    def last(row):
        for m in range(parts_m):
            at = slice(m * SUB, (m + 1) * SUB)
            values = [ref[row + off, at, :] for ref, off in d_refs + r_refs]
            total[row, at, :] = total[row, at, :] + combined(x_at, values, at)
            dirs[row + S, at, :] = combined(r_at, values, at)

    chunk = rows // 2
    writes = []
    for index in range(2):
        over_rows(index * chunk, (index + 1) * chunk, last)
        rng = pl.ds(index * chunk, chunk)
        copy = pltpu.make_async_copy(total.at[rng], sol_ref.at[rng], local_sems.at[1 + 2 * index])
        copy.start()
        writes.append(copy)
        copy = pltpu.make_async_copy(dirs.at[pl.ds(S + index * chunk, chunk)], res_ref.at[rng], local_sems.at[2 + 2 * index])
        copy.start()
        writes.append(copy)

    for slot in range(slots):
        @pl.when(tile > 0)
        def _(slot=slot):
            halo_copy(0, slot).wait_send()

        @pl.when(tile < tiles - 1)
        def _(slot=slot):
            halo_copy(1, slot).wait_send()
    for copy in writes:
        copy.wait()


def shards(increments, projection, helmholtz):
    tiles, levs = lax.axis_size("tile"), lax.axis_size("lev")
    own_levels, rows, cells = increments.shape
    modes = projection.shape[0] // levs
    levels = own_levels * levs
    groups = stage_groups(tiles)
    most = max(groups)
    slots = HALO // 2
    vmem = pltpu.VMEM
    dma = pltpu.SemaphoreType.DMA
    scratch = [
        vmem((levs, own_levels * rows, cells), bf16),
        vmem((levs, rows * modes, own_levels * rows), bf16),
        vmem((S + 1, rows + 2 * HALO, modes, cells), f32),
        vmem((rows + 2 * S, modes, cells), f32),
        vmem((rows + 2 * S, modes, cells), f32),
        vmem((S - 2, rows + 2 * S, modes, cells), f32),
        vmem((rows, modes, cells), f32),
        vmem((2, slots, 2 * modes, cells), bf16),
        vmem((2, slots, 2 * modes, cells), bf16),
        vmem((3, modes, LANE), f32),
        vmem((6 * S, modes, LANE), f32),
        vmem((6 * S, modes, LANE), f32),
        vmem((2, len(groups), most, modes, LANE), f32),
        dma((5,)),
        dma((levs - 1,)),
        dma((levs - 1,)),
        dma((2, slots)),
        dma((2, slots)),
        dma((2, len(groups), most)),
        dma((2, len(groups), most)),
    ]
    shape = jax.ShapeDtypeStruct((rows, modes, cells), f32)
    solved, resid = pl.pallas_call(
        functools.partial(kernel, tiles, levs, groups, rows, modes, cells, levels),
        out_shape=(shape, shape),
        in_specs=[pl.BlockSpec(memory_space=pl.ANY), pl.BlockSpec(memory_space=pltpu.VMEM),
                  pl.BlockSpec(memory_space=pltpu.VMEM)],
        out_specs=(pl.BlockSpec(memory_space=pl.ANY), pl.BlockSpec(memory_space=pl.ANY)),
        scratch_shapes=scratch,
        compiler_params=pltpu.CompilerParams(collective_id=0, has_side_effects=True, vmem_limit_bytes=67000000),
    )(increments.reshape(own_levels * rows, cells), projection, helmholtz.reshape(1, modes))
    return jnp.transpose(solved, (1, 0, 2)), jnp.transpose(resid, (1, 0, 2))


def solution(mesh):
    in_specs = (P("lev", "tile", None), P(), P("lev"))
    out_specs = (P("lev", "tile", None), P("lev", "tile", None))
    return jax.shard_map(shards, mesh=mesh, in_specs=in_specs, out_specs=out_specs, check_vma=False)
```

profile of v0, /device:TPU:0, one launch (start us, length us, event | category | flops | bytes accessed | tf_op | source)
XLA Modules:
  0.0 100.3 jit_solution(4801404587069478540)
XLA Ops:
  0.6 1.5 %copy.5.proj_ref = bf16[80,136]{1,0:T(8,128)(2,1)} copy(bf16[80,136]{0,1:T(8,128)(2,1)} %param.4) | data formatting | bytes 43520 | tf_op args[1]
  2.1 90.2 %shard_map.50 = (f32[16,40,1024]{2,1,0:T(8,128)}, f32[16,40,1024]{2,1,0:T(8,128)}) custom-call(bf16[1088,1024]{1,0:T(8,128)(2,1)} %bitcast.6, bf16[80,136]{1,0:T(8,128)(2,1)} %copy.5.proj_ref, f32[1,40]{1,0:T(1,128)} %bitcast.7), custom_call_target="tpu_custom_call" | custom-call | tf_op jit(solution)/shard_map/pallas_call | solution.py:526
  92.3 0.0 copy-start
  92.3 4.9 %copy.6 = f32[40,16,1024]{2,1,0:T(8,128)} copy(f32[40,16,1024]{2,0,1:T(8,128)} %bitcast.5) | data formatting | bytes 5242880
  97.2 0.0 copy-done
  97.2 3.0 %copy.7 = f32[40,16,1024]{2,1,0:T(8,128)} copy(f32[40,16,1024]{2,0,1:T(8,128)S(1)} %bitcast.4) | data formatting | bytes 5242880
Async XLA Ops:
  92.3 4.9 %copy-start = (f32[16,40,1024]{2,1,0:T(8,128)S(1)}, f32[16,40,1024]{2,1,0:T(8,128)}, u32[]{:S(2)}) copy-start(f32[16,40,1024]{2,1,0:T(8,128)} %get-tuple-element.5) | copy-start | bytes 7864324
where the time goes:
time: 101 us; the launch traced here: 100 us
  Pallas kernels  90.2 us (89%)
  local copies, waits for them, and re-layouts  9.39 us (9%)
    pallas_call x1, Pallas kernels, shards(): pl.pallas_call(functools.partial(kernel, tiles, levs, groups, rows, modes...  90.2 us
    unnamed x5, local copies, waits for them, and re-layouts  9.39 us

commit v1 on v0

v1 whole, which is shorter than its diff:
```python
import functools

import jax
import jax.numpy as jnp
from jax import lax
from jax.experimental import pallas as pl
from jax.experimental.pallas import tpu as pltpu
from jax.sharding import PartitionSpec as P

STEPS = 8
HALO = STEPS
HALF = HALO // 2
POWER = 13
SUB = 8
LANE = 128
CHUNKS = 4
MESH = pl.DeviceIdType.MESH
f32 = jnp.float32
bf16 = jnp.bfloat16


def stage_groups(count):
    groups = []
    while count > 1:
        size = next(size for size in (16, 4, 2, count) if count % size == 0)
        groups.append(size)
        count //= size
    return groups


def encode(value, scale):
    a = value * scale
    a4 = (a * a) * (a * a)
    return ((a4 * a4) * (a4 * a)).astype(bf16)


def decode(code, scale):
    code = code.astype(f32)
    size = jnp.exp(jnp.log(jnp.maximum(jnp.abs(code), 2.0 ** -126)) * (1.0 / POWER)) * (1.0 / scale)
    return jnp.where(code > 0.0, size, jnp.where(code < 0.0, -size, 0.0))


def add(left, right):
    if left is None:
        return right
    if right is None:
        return left
    return left + right


def coefficients(products, theta):
    count = 2 * STEPS
    moments = list(products[:2])
    for index in range(2, count):
        moments.append(products[index] + products[index] - moments[index % 2])
    half = 0.5 * theta
    one = jnp.ones_like(theta)
    x, r, p = [None] * STEPS, [one], [one]
    r_moments, p_moments = list(moments), list(moments)
    for step in range(STEPS):
        low, high = step, count - 1 - step
        image = {}
        for l in range(low, high):
            if l == 0:
                image[l] = p_moments[0] - theta * p_moments[1]
            else:
                image[l] = p_moments[l] - half * (p_moments[l + 1] + p_moments[l - 1])
        alpha = r_moments[step] / image[step]
        for k in range(step + 1):
            x[k] = add(x[k], alpha * p[k])
        gain = alpha * half
        twice = alpha * theta
        fresh = []
        for k in range(step + 2):
            value = r[k] if k < len(r) else None
            if k < len(p):
                value = value - alpha * p[k] if value is not None else -(alpha * p[k])
            if k == 1:
                value = add(value, twice * p[0])
            elif k > 1:
                value = add(value, gain * p[k - 1])
            if k + 1 < len(p):
                value = value + gain * p[k + 1]
            fresh.append(value)
        r = fresh
        if step == STEPS - 1:
            break
        old = r_moments[step]
        r_moments = [r_moments[l] - alpha * image[l] if l in image else None for l in range(count)]
        beta = (twice if step == 0 else gain) * r_moments[step + 1] / old
        p = [r[k] + beta * p[k] if k < len(p) else r[k] for k in range(step + 2)]
        p_moments = [r_moments[l] + beta * p_moments[l] if l in image else None for l in range(count)]
    return x, r


def kernel(tiles, levs, groups, rows, modes, cells, levels, inc_ref, proj_ref, helm_ref, sol_ref, res_ref,
           x_all, wide, base, powers, out_buf, in_buf, results, thetas, sums, grams,
           local_sem, swap_send, swap_recv, halo_send, halo_recv, gram_send, gram_recv, write_sems):
    tile = lax.axis_index("tile")
    lev = lax.axis_index("lev")
    part = inc_ref.shape[0]
    across = cells // LANE
    parts = modes // SUB
    barrier = pltpu.get_barrier_semaphore()

    stage_peers = []
    stride = 1
    for size in groups:
        digit = lax.rem(lax.div(tile, stride), size)
        start = tile - digit * stride
        stage_peers.append((digit, [start + lax.rem(digit + j, size) * stride for j in range(1, size)]))
        stride *= size

    count = 0
    for j in range(1, levs):
        pl.semaphore_signal(barrier, 1, device_id=(tile, lax.rem(lev + j, levs)), device_id_type=MESH)
        count += 1
    for peer in (lax.rem(tile + 1, tiles), lax.rem(tile + tiles - 1, tiles)):
        pl.semaphore_signal(barrier, 1, device_id=(peer, lev), device_id_type=MESH)
        count += 1
    for digit, peers in stage_peers:
        for peer in peers:
            pl.semaphore_signal(barrier, 1, device_id=(peer, lev), device_id_type=MESH)
            count += 1

    local = pltpu.make_async_copy(inc_ref, x_all.at[0], local_sem)
    local.start()

    chunk = cells // CHUNKS
    with jax.named_scope("barrier"):
        pl.semaphore_wait(barrier, count)

    def swap(j, c):
        cols = pl.ds(c * chunk, chunk)
        return pltpu.make_async_remote_copy(
            src_ref=inc_ref.at[:, cols], dst_ref=x_all.at[levs - j, :, cols], send_sem=swap_send.at[j - 1, c],
            recv_sem=swap_recv.at[j - 1, c], device_id=(tile, lax.rem(lev + j, levs)), device_id_type=MESH)

    for c in range(CHUNKS):
        for j in range(1, levs):
            swap(j, c).start()

    proj = proj_ref[...].astype(f32)
    own = proj[0:modes]
    for j in range(1, levs):
        own = jnp.where(lev == j, proj[j * modes:(j + 1) * modes], own)
    own_levels = levels // levs
    groups_l = [own[:, j * own_levels:(j + 1) * own_levels] for j in range(levs)]
    col_e = lax.broadcasted_iota(jnp.int32, (own_levels, part), 1)
    row_e = lax.broadcasted_iota(jnp.int32, (own_levels, part), 0) * rows
    onehot = jnp.where((col_e >= row_e) & (col_e < row_e + rows), 1.0, 0.0).astype(bf16)
    col_w = lax.rem(lax.broadcasted_iota(jnp.int32, (2 * modes, part), 1), rows)
    second = jnp.where(lax.broadcasted_iota(jnp.int32, (2 * modes, part), 0) >= modes, 1, 0)
    pick = col_w - second

    def widen(position):
        chosen = groups_l[position]
        for j in range(1, levs):
            chosen = jnp.where(lev == j, groups_l[(j + position) % levs], chosen)
        twice = jnp.concatenate([chosen, chosen], axis=0).astype(bf16)
        repeated = jnp.dot(twice, onehot, preferred_element_type=f32)
        for pair in range(rows // 2):
            wide[position, pair * 2 * modes:(pair + 1) * 2 * modes, :] = jnp.where(
                pick == 2 * pair, repeated, 0.0).astype(bf16)

    def project(position, c):
        cols = slice(c * chunk, (c + 1) * chunk)
        got = jnp.dot(wide[position], x_all[position, :, cols], preferred_element_type=f32)
        got = got.reshape(rows, parts, SUB, chunk)
        for g in range(parts):
            value = got[:, g]
            if position:
                value = base[g, HALO:HALO + rows, :, cols] + value
            base[g, HALO:HALO + rows, :, cols] = value

    with jax.named_scope("widen"):
        widen(0)
    with jax.named_scope("own"):
        local.wait()
        for c in range(CHUNKS):
            project(0, c)
    with jax.named_scope("widen"):
        for j in range(1, levs):
            widen(j)

    diag = lax.broadcasted_iota(jnp.int32, (modes, modes), 0) == lax.broadcasted_iota(jnp.int32, (modes, modes), 1)
    helm = jnp.sum(jnp.where(diag, jnp.broadcast_to(helm_ref[...], (modes, modes)), 0.0), axis=1, keepdims=True)
    thetas[...] = jnp.broadcast_to(4.0 / (4.0 + helm), (modes, LANE))
    has = {0: tile < tiles - 1, 1: tile > 0}
    for side in range(2):
        @pl.when(jnp.logical_not(has[side]))
        def _(side=side):
            in_buf[:, side] = jnp.zeros_like(in_buf[:, side])

    scale = 2.0 ** 9.7 / (0.5 * 30.0 * levels)

    def halo_first(side, half):
        if side == 0:
            return half * HALF
        return rows - (half + 1) * HALF

    def halo_copy(g, side, half):
        peer = lax.rem(tile + tiles - 1, tiles) if side == 0 else lax.rem(tile + 1, tiles)
        return pltpu.make_async_remote_copy(
            src_ref=out_buf.at[g, side, half], dst_ref=in_buf.at[g, side, half], send_sem=halo_send.at[g, side, half],
            recv_sem=halo_recv.at[g, side, half], device_id=(peer, lev), device_id_type=MESH)

    sends = {0: tile > 0, 1: tile < tiles - 1}

    def encode_part(g, half, side, cols):
        first = HALO + halo_first(side, half)
        width = cols.stop - cols.start
        out_buf[g, side, half, :, cols] = encode(base[g, first:first + HALF, :, cols].reshape(HALF * SUB, width), scale)

    def send_part(g, half, side):
        @pl.when(sends[side])
        def _():
            halo_copy(g, side, half).start()

    with jax.named_scope("other"):
        for c in range(CHUNKS):
            for j in range(1, levs):
                swap(j, c).wait_recv()
                project(j, c)
            cols = slice(c * chunk, (c + 1) * chunk)
            for half in range(2):
                for side in range(2):
                    encode_part(0, half, side, cols)
    with jax.named_scope("send"):
        for g in range(parts):
            for half in range(2):
                for side in range(2):
                    if g:
                        encode_part(g, half, side, slice(0, cells))
                    send_part(g, half, side)

    lane = lax.broadcasted_iota(jnp.int32, (SUB, LANE), 1)
    first_lane = lane == 0
    last_lane = lane == LANE - 1
    nothing = jnp.zeros((SUB, LANE), f32)

    def beside(tile_row):
        pieces = [tile_row[:, j * LANE:(j + 1) * LANE] for j in range(across)]
        right = [pltpu.roll(piece, 1, 1) for piece in pieces]
        left = [pltpu.roll(piece, LANE - 1, 1) for piece in pieces]
        result = []
        for j in range(across):
            low = jnp.where(first_lane, right[j - 1] if j else nothing, right[j])
            high = jnp.where(last_lane, left[j + 1] if j + 1 < across else nothing, left[j])
            result.append(low + high)
        return jnp.concatenate(result, axis=1)

    def fold(product):
        pieces = [product[:, j * LANE:(j + 1) * LANE] for j in range(across)]
        while len(pieces) > 1:
            pieces = [pieces[i] + pieces[i + 1] if i + 1 < len(pieces) else pieces[i] for i in range(0, len(pieces), 2)]
        return pieces[0]

    inside = jnp.float32(0.5)
    factor = {0: jnp.where(tile > 0, inside, 0.0), 1: jnp.where(tile < tiles - 1, inside, 0.0)}

    def field(g, k):
        return base.at[g] if k == 0 else powers.at[g % 2, k - 1]

    def extend(g, k, ranges):
        src, dst = field(g, k - 1), field(g, k)
        before = field(g, k - 2) if k > 1 else None
        totals = {}
        for low, high in ranges:
            for row in range(low, high):
                at = row + HALO
                here = src[at]
                around = src[at - 1] + src[at + 1] + beside(here)
                if row < 0:
                    gain = factor[0]
                elif row >= rows:
                    gain = factor[1]
                else:
                    gain = 0.5
                if k == 1:
                    gain = gain * 0.5
                fresh = gain * around
                if before is not None:
                    fresh = fresh - before[at]
                dst[at] = fresh
                if 0 <= row < rows:
                    if k == 1:
                        totals[0] = add(totals.get(0), fold(here * here))
                    totals[2 * k - 1] = add(totals.get(2 * k - 1), fold(here * fresh))
                    if k < STEPS:
                        totals[2 * k] = add(totals.get(2 * k), fold(fresh * fresh))
        for slot, value in totals.items():
            sums[slot] = sums[slot] + value

    def interior(g):
        with jax.named_scope("interior"):
            for k in range(1, STEPS):
                if rows - k > k:
                    extend(g, k, [(k, rows - k)])

    def take(g, half):
        with jax.named_scope("take"):
            for side in range(2):
                @pl.when(has[side])
                def _(side=side):
                    halo_copy(g, side, half).wait_recv()
        with jax.named_scope("decode"):
            for side in range(2):
                if side == 0:
                    first = HALO + rows + half * HALF
                else:
                    first = HALO - (half + 1) * HALF
                base[g, first:first + HALF] = decode(in_buf[g, side, half], scale).reshape(HALF, SUB, cells)

    def outer(g, half):
        with jax.named_scope("outer"):
            old, new = half * HALF, (half + 1) * HALF
            for k in range(1, STEPS + 1):
                if rows - k + old >= k - old:
                    extend(g, k, [(k - new, k - old), (rows - k + old, rows - k + new)])
                else:
                    middle = rows // 2
                    extend(g, k, [(k - new, middle), (middle, rows - k + new)])

    products = 2 * STEPS

    def gram_copies(g, stage):
        digit, peers = stage_peers[stage]
        return [pltpu.make_async_remote_copy(
            src_ref=grams.at[g, stage, digit], dst_ref=grams.at[g, stage, digit],
            send_sem=gram_send.at[g, stage, j], recv_sem=gram_recv.at[g, stage, digit],
            device_id=(peer, lev), device_id_type=MESH) for j, peer in enumerate(peers)]

    def gram_start(g, stage, table):
        grams[g, stage, stage_peers[stage][0]] = table
        for copy in gram_copies(g, stage):
            copy.start()

    def gram_finish(g, stage):
        digit, peers = stage_peers[stage]
        size = groups[stage]
        for copy in gram_copies(g, stage):
            copy.wait_send()
        for j in range(1, size):
            sender = lax.rem(digit + j, size)
            pltpu.make_async_remote_copy(
                src_ref=grams.at[g, stage, sender], dst_ref=grams.at[g, stage, sender],
                send_sem=gram_send.at[g, stage, j - 1], recv_sem=gram_recv.at[g, stage, sender],
                device_id=(peers[j - 1], lev), device_id_type=MESH).wait_recv()
        tables = [grams[g, stage, j] for j in range(size)]
        while len(tables) > 1:
            tables = [tables[i] + tables[i + 1] if i + 1 < len(tables) else tables[i] for i in range(0, len(tables), 2)]
        return tables[0]

    def total(g):
        with jax.named_scope("total"):
            lanes = lax.broadcasted_iota(jnp.int32, (SUB, LANE), 1)
            table = jnp.zeros((SUB, LANE), f32)
            for slot in range(products):
                table = jnp.where(lanes == slot, jnp.sum(sums[slot], axis=1, keepdims=True), table)
            sums[...] = jnp.zeros_like(sums)
            gram_start(g, 0, table)

    def finish(g):
        with jax.named_scope("gram"):
            for stage in range(len(groups)):
                table = gram_finish(g, stage)
                if stage + 1 < len(groups):
                    gram_start(g, stage + 1, table)
        with jax.named_scope("coef"):
            columns = [jnp.broadcast_to(table[:, slot:slot + 1], (SUB, LANE)) for slot in range(products)]
            x, r = coefficients(columns, thetas[g * SUB:(g + 1) * SUB])
        with jax.named_scope("combine"):
            for row in range(rows):
                at = row + HALO
                solved, left = [], []
                for j in range(across):
                    cols = slice(j * LANE, (j + 1) * LANE)
                    x_sum = r_sum = None
                    for k in range(STEPS + 1):
                        value = field(g, k)[at, :, cols]
                        r_sum = add(r_sum, r[k] * value)
                        if k < STEPS:
                            x_sum = add(x_sum, x[k] * value)
                    solved.append(x_sum)
                    left.append(r_sum)
                results[g, 0, :, row, :] = jnp.concatenate(solved, axis=1)
                results[g, 1, :, row, :] = jnp.concatenate(left, axis=1)
        for out, ref in enumerate((sol_ref, res_ref)):
            pltpu.make_async_copy(results.at[g, out], ref.at[pl.ds(g * SUB, SUB)], write_sems.at[g, out]).start()

    sums[...] = jnp.zeros_like(sums)
    for g in range(parts):
        interior(g)
        if g:
            finish(g - 1)
        for half in range(2):
            take(g, half)
            outer(g, half)
        total(g)
    finish(parts - 1)

    with jax.named_scope("drain"):
        for j in range(1, levs):
            for c in range(CHUNKS):
                swap(j, c).wait_send()
        for g in range(parts):
            for half in range(2):
                for side in range(2):
                    @pl.when(sends[side])
                    def _(g=g, side=side, half=half):
                        halo_copy(g, side, half).wait_send()
        for g in range(parts):
            for out, ref in enumerate((sol_ref, res_ref)):
                pltpu.make_async_copy(results.at[g, out], ref.at[pl.ds(g * SUB, SUB)], write_sems.at[g, out]).wait()


def shards(increments, projection, helmholtz):
    tiles, levs = lax.axis_size("tile"), lax.axis_size("lev")
    own_levels, rows, cells = increments.shape
    modes = projection.shape[0] // levs
    levels = own_levels * levs
    groups = stage_groups(tiles)
    most = max(groups)
    parts = modes // SUB
    vmem = pltpu.VMEM
    dma = pltpu.SemaphoreType.DMA
    scratch = [
        vmem((levs, own_levels * rows, cells), bf16),
        vmem((levs, rows * modes, own_levels * rows), bf16),
        vmem((parts, rows + 2 * HALO, SUB, cells), f32),
        vmem((2, STEPS, rows + 2 * HALO, SUB, cells), f32),
        vmem((parts, 2, 2, HALF * SUB, cells), bf16),
        vmem((parts, 2, 2, HALF * SUB, cells), bf16),
        vmem((parts, 2, SUB, rows, cells), f32),
        vmem((modes, LANE), f32),
        vmem((2 * STEPS, SUB, LANE), f32),
        vmem((parts, len(groups), most, SUB, LANE), f32),
        dma,
        dma((levs - 1, CHUNKS)),
        dma((levs - 1, CHUNKS)),
        dma((parts, 2, 2)),
        dma((parts, 2, 2)),
        dma((parts, len(groups), most)),
        dma((parts, len(groups), most)),
        dma((parts, 2)),
    ]
    shape = jax.ShapeDtypeStruct((modes, rows, cells), f32)
    return pl.pallas_call(
        functools.partial(kernel, tiles, levs, groups, rows, modes, cells, levels),
        out_shape=(shape, shape),
        in_specs=[pl.BlockSpec(memory_space=pl.ANY), pl.BlockSpec(memory_space=pltpu.VMEM),
                  pl.BlockSpec(memory_space=pltpu.VMEM)],
        out_specs=(pl.BlockSpec(memory_space=pl.ANY), pl.BlockSpec(memory_space=pl.ANY)),
        scratch_shapes=scratch,
        compiler_params=pltpu.CompilerParams(collective_id=0, has_side_effects=True, vmem_limit_bytes=67000000),
    )(increments.reshape(own_levels * rows, cells), projection, helmholtz.reshape(1, modes))


def solution(mesh):
    in_specs = (P("lev", "tile", None), P(), P("lev"))
    out_specs = (P("lev", "tile", None), P("lev", "tile", None))
    return jax.shard_map(shards, mesh=mesh, in_specs=in_specs, out_specs=out_specs, check_vma=False)
```

time: 101 us -> 88.9 us (0.88)
  Pallas kernels: 90.2 us -> 81.3 us
  local copies, waits for them, and re-layouts: 9.39 us -> 6.68 us
    pallas_call x1, Pallas kernels: 90.2 us -> 81.3 us  [shards(): pl.pallas_call(functools.partial(kernel, tiles, levs, groups, rows, modes...]
    unnamed x5, local copies, waits for them, and re-layouts: 9.39 us -> 6.68 us
where the time goes in v1:
time: 88.9 us; the launch traced here: 88.7 us
  Pallas kernels  81.3 us (91%)
  local copies, waits for them, and re-layouts  6.68 us (8%)
    pallas_call x1, Pallas kernels, shards(): pl.pallas_call(functools.partial(kernel, tiles, levs, groups, rows, modes...  81.3 us
    unnamed x5, local copies, waits for them, and re-layouts  6.68 us

profile of v1, /device:TPU:0, one launch (start us, length us, event | category | flops | bytes accessed | tf_op | source)
XLA Modules:
  0.0 88.7 jit_solution(15281117065301253628)
XLA Ops:
  0.6 1.5 %copy.5.proj_ref = bf16[80,136]{1,0:T(8,128)(2,1)} copy(bf16[80,136]{0,1:T(8,128)(2,1)} %param.4) | data formatting | bytes 43520 | tf_op args[1]
  2.1 81.3 %shard_map.50 = (f32[40,16,1024]{2,1,0:T(8,128)}, f32[40,16,1024]{2,1,0:T(8,128)}) custom-call(bf16[1088,1024]{1,0:T(8,128)(2,1)} %bitcast.2, bf16[80,136]{1,0:T(8,128)(2,1)} %copy.5.proj_ref, f32[1,40]{1,0:T(1,128)} %bitcast.3), custom_call_target="tpu_custom_call" | custom-call | tf_op jit(solution)/shard_map/pallas_call | solution.py:449
  83.4 0.0 copy-start
  83.4 3.7 %copy.8 = f32[40,16,1024]{2,1,0:T(8,128)} copy(f32[40,16,1024]{2,1,0:T(8,128)} %get-tuple-element.4) | data formatting | bytes 5242880
  87.2 0.0 copy-done
  87.2 1.5 %copy.9 = f32[40,16,1024]{2,1,0:T(8,128)} copy(f32[40,16,1024]{2,1,0:T(8,128)S(1)} %copy-done) | data formatting | bytes 5242880
Async XLA Ops:
  83.4 3.7 %copy-start = (f32[40,16,1024]{2,1,0:T(8,128)S(1)}, f32[40,16,1024]{2,1,0:T(8,128)}, u32[]{:S(2)}) copy-start(f32[40,16,1024]{2,1,0:T(8,128)} %get-tuple-element.5) | copy-start | bytes 7864324

commit v2 on v1

--- a/solution.py
+++ b/solution.py
@@ -12,6 +12,8 @@
 HALF = HALO // 2
 POWER = 13
 SUB = 8
+RING = 3
+LAG = 2
 LANE = 128
 CHUNKS = 4
 MESH = pl.DeviceIdType.MESH
@@ -94,8 +96,8 @@
 
 
 def kernel(tiles, levs, groups, rows, modes, cells, levels, inc_ref, proj_ref, helm_ref, sol_ref, res_ref,
-           x_all, wide, base, powers, out_buf, in_buf, results, thetas, sums, grams,
-           local_sem, swap_send, swap_recv, halo_send, halo_recv, gram_send, gram_recv, write_sems):
+           x_all, wide, base, powers, out_buf, in_buf, thetas, sums, grams,
+           local_sem, swap_send, swap_recv, halo_send, halo_recv, gram_send, gram_recv):
     tile = lax.axis_index("tile")
     lev = lax.axis_index("lev")
     part = inc_ref.shape[0]
@@ -141,11 +143,11 @@
             swap(j, c).start()
 
     proj = proj_ref[...].astype(f32)
-    own = proj[0:modes]
+    own = proj[:, 0:modes]
     for j in range(1, levs):
-        own = jnp.where(lev == j, proj[j * modes:(j + 1) * modes], own)
+        own = jnp.where(lev == j, proj[:, j * modes:(j + 1) * modes], own)
     own_levels = levels // levs
-    groups_l = [own[:, j * own_levels:(j + 1) * own_levels] for j in range(levs)]
+    groups_l = [own[j * own_levels:(j + 1) * own_levels] for j in range(levs)]
     col_e = lax.broadcasted_iota(jnp.int32, (own_levels, part), 1)
     row_e = lax.broadcasted_iota(jnp.int32, (own_levels, part), 0) * rows
     onehot = jnp.where((col_e >= row_e) & (col_e < row_e + rows), 1.0, 0.0).astype(bf16)
@@ -157,8 +159,8 @@
         chosen = groups_l[position]
         for j in range(1, levs):
             chosen = jnp.where(lev == j, groups_l[(j + position) % levs], chosen)
-        twice = jnp.concatenate([chosen, chosen], axis=0).astype(bf16)
-        repeated = jnp.dot(twice, onehot, preferred_element_type=f32)
+        twice = jnp.concatenate([chosen, chosen], axis=1).astype(bf16)
+        repeated = lax.dot_general(twice, onehot, (((0,), (0,)), ((), ())), preferred_element_type=f32)
         for pair in range(rows // 2):
             wide[position, pair * 2 * modes:(pair + 1) * 2 * modes, :] = jnp.where(
                 pick == 2 * pair, repeated, 0.0).astype(bf16)
@@ -199,10 +201,10 @@
             return half * HALF
         return rows - (half + 1) * HALF
 
-    def halo_copy(g, side, half):
+    def halo_copy(g, side, half, cols=slice(None)):
         peer = lax.rem(tile + tiles - 1, tiles) if side == 0 else lax.rem(tile + 1, tiles)
         return pltpu.make_async_remote_copy(
-            src_ref=out_buf.at[g, side, half], dst_ref=in_buf.at[g, side, half], send_sem=halo_send.at[g, side, half],
+            src_ref=out_buf.at[g, side, half, :, cols], dst_ref=in_buf.at[g, side, half, :, cols], send_sem=halo_send.at[g, side, half],
             recv_sem=halo_recv.at[g, side, half], device_id=(peer, lev), device_id_type=MESH)
 
     sends = {0: tile > 0, 1: tile < tiles - 1}
@@ -212,27 +214,34 @@
         width = cols.stop - cols.start
         out_buf[g, side, half, :, cols] = encode(base[g, first:first + HALF, :, cols].reshape(HALF * SUB, width), scale)
 
-    def send_part(g, half, side):
-        @pl.when(sends[side])
-        def _():
-            halo_copy(g, side, half).start()
+    def send_chunk(c):
+        cols = pl.ds(c * chunk, chunk)
+        for half in range(2):
+            for side in range(2):
+                encode_part(0, half, side, slice(c * chunk, (c + 1) * chunk))
+
+                @pl.when(sends[side])
+                def _(half=half, side=side):
+                    halo_copy(0, side, half, cols).start()
+
+    def send(g):
+        with jax.named_scope("send"):
+            for half in range(2):
+                for side in range(2):
+                    encode_part(g, half, side, slice(0, cells))
+
+                    @pl.when(sends[side])
+                    def _(half=half, side=side):
+                        halo_copy(g, side, half).start()
 
     with jax.named_scope("other"):
         for c in range(CHUNKS):
             for j in range(1, levs):
                 swap(j, c).wait_recv()
                 project(j, c)
-            cols = slice(c * chunk, (c + 1) * chunk)
-            for half in range(2):
-                for side in range(2):
-                    encode_part(0, half, side, cols)
-    with jax.named_scope("send"):
-        for g in range(parts):
-            for half in range(2):
-                for side in range(2):
-                    if g:
-                        encode_part(g, half, side, slice(0, cells))
-                    send_part(g, half, side)
+            send_chunk(c)
+    if parts > 1:
+        send(1)
 
     lane = lax.broadcasted_iota(jnp.int32, (SUB, LANE), 1)
     first_lane = lane == 0
@@ -260,7 +269,7 @@
     factor = {0: jnp.where(tile > 0, inside, 0.0), 1: jnp.where(tile < tiles - 1, inside, 0.0)}
 
     def field(g, k):
-        return base.at[g] if k == 0 else powers.at[g % 2, k - 1]
+        return base.at[g] if k == 0 else powers.at[lax.rem(g, RING), k - 1]
 
     def extend(g, k, ranges):
         src, dst = field(g, k - 1), field(g, k)
@@ -316,37 +325,28 @@
         with jax.named_scope("outer"):
             old, new = half * HALF, (half + 1) * HALF
             for k in range(1, STEPS + 1):
-                if rows - k + old >= k - old:
-                    extend(g, k, [(k - new, k - old), (rows - k + old, rows - k + new)])
-                else:
-                    middle = rows // 2
-                    extend(g, k, [(k - new, middle), (middle, rows - k + new)])
+                extend(g, k, [(k - new, k - old), (rows - k + old, rows - k + new)])
 
     products = 2 * STEPS
 
-    def gram_copies(g, stage):
+    def modes_of(g):
+        return pl.ds(pl.multiple_of(g * SUB, SUB), SUB)
+
+    def gram_start(g, stage, table):
         digit, peers = stage_peers[stage]
-        return [pltpu.make_async_remote_copy(
-            src_ref=grams.at[g, stage, digit], dst_ref=grams.at[g, stage, digit],
-            send_sem=gram_send.at[g, stage, j], recv_sem=gram_recv.at[g, stage, digit],
-            device_id=(peer, lev), device_id_type=MESH) for j, peer in enumerate(peers)]
-
-    def gram_start(g, stage, table):
-        grams[g, stage, stage_peers[stage][0]] = table
-        for copy in gram_copies(g, stage):
-            copy.start()
+        grams[g, stage, digit] = table
+        for peer in peers:
+            pltpu.make_async_remote_copy(
+                src_ref=grams.at[g, stage, digit], dst_ref=grams.at[g, stage, digit], send_sem=gram_send.at[g, stage],
+                recv_sem=gram_recv.at[g, stage], device_id=(peer, lev), device_id_type=MESH).start()
 
     def gram_finish(g, stage):
         digit, peers = stage_peers[stage]
         size = groups[stage]
-        for copy in gram_copies(g, stage):
-            copy.wait_send()
-        for j in range(1, size):
-            sender = lax.rem(digit + j, size)
-            pltpu.make_async_remote_copy(
-                src_ref=grams.at[g, stage, sender], dst_ref=grams.at[g, stage, sender],
-                send_sem=gram_send.at[g, stage, j - 1], recv_sem=gram_recv.at[g, stage, sender],
-                device_id=(peers[j - 1], lev), device_id_type=MESH).wait_recv()
+        others = grams.at[g, stage, pl.ds(0, size - 1)]
+        pltpu.make_async_remote_copy(
+            src_ref=others, dst_ref=others, send_sem=gram_send.at[g, stage],
+            recv_sem=gram_recv.at[g, stage], device_id=(peers[0], lev), device_id_type=MESH).wait()
         tables = [grams[g, stage, j] for j in range(size)]
         while len(tables) > 1:
             tables = [tables[i] + tables[i + 1] if i + 1 < len(tables) else tables[i] for i in range(0, len(tables), 2)]
@@ -369,7 +369,7 @@
                     gram_start(g, stage + 1, table)
         with jax.named_scope("coef"):
             columns = [jnp.broadcast_to(table[:, slot:slot + 1], (SUB, LANE)) for slot in range(products)]
-            x, r = coefficients(columns, thetas[g * SUB:(g + 1) * SUB])
+            x, r = coefficients(columns, thetas[modes_of(g)])
         with jax.named_scope("combine"):
             for row in range(rows):
                 at = row + HALO
@@ -384,21 +384,31 @@
                             x_sum = add(x_sum, x[k] * value)
                     solved.append(x_sum)
                     left.append(r_sum)
-                results[g, 0, :, row, :] = jnp.concatenate(solved, axis=1)
-                results[g, 1, :, row, :] = jnp.concatenate(left, axis=1)
-        for out, ref in enumerate((sol_ref, res_ref)):
-            pltpu.make_async_copy(results.at[g, out], ref.at[pl.ds(g * SUB, SUB)], write_sems.at[g, out]).start()
+                sol_ref[modes_of(g), row, :] = jnp.concatenate(solved, axis=1)
+                res_ref[modes_of(g), row, :] = jnp.concatenate(left, axis=1)
 
     sums[...] = jnp.zeros_like(sums)
-    for g in range(parts):
-        interior(g)
-        if g:
-            finish(g - 1)
-        for half in range(2):
-            take(g, half)
-            outer(g, half)
-        total(g)
-    finish(parts - 1)
+
+    def advance(index, carry):
+        @pl.when(index < parts)
+        def _():
+            interior(index)
+            for half in range(2):
+                take(index, half)
+                outer(index, half)
+            total(index)
+
+        @pl.when(index + LAG < parts)
+        def _():
+            send(index + LAG)
+
+        @pl.when(index >= LAG)
+        def _():
+            finish(index - LAG)
+
+        return carry
+
+    lax.fori_loop(0, parts + LAG, advance, 0)
 
     with jax.named_scope("drain"):
         for j in range(1, levs):
@@ -410,9 +420,6 @@
                     @pl.when(sends[side])
                     def _(g=g, side=side, half=half):
                         halo_copy(g, side, half).wait_send()
-        for g in range(parts):
-            for out, ref in enumerate((sol_ref, res_ref)):
-                pltpu.make_async_copy(results.at[g, out], ref.at[pl.ds(g * SUB, SUB)], write_sems.at[g, out]).wait()
 
 
 def shards(increments, projection, helmholtz):
@@ -429,10 +436,9 @@
         vmem((levs, own_levels * rows, cells), bf16),
         vmem((levs, rows * modes, own_levels * rows), bf16),
         vmem((parts, rows + 2 * HALO, SUB, cells), f32),
-        vmem((2, STEPS, rows + 2 * HALO, SUB, cells), f32),
+        vmem((RING, STEPS, rows + 2 * HALO, SUB, cells), f32),
         vmem((parts, 2, 2, HALF * SUB, cells), bf16),
         vmem((parts, 2, 2, HALF * SUB, cells), bf16),
-        vmem((parts, 2, SUB, rows, cells), f32),
         vmem((modes, LANE), f32),
         vmem((2 * STEPS, SUB, LANE), f32),
         vmem((parts, len(groups), most, SUB, LANE), f32),
@@ -441,20 +447,19 @@
         dma((levs - 1, CHUNKS)),
         dma((parts, 2, 2)),
         dma((parts, 2, 2)),
-        dma((parts, len(groups), most)),
-        dma((parts, len(groups), most)),
-        dma((parts, 2)),
+        dma((parts, len(groups))),
+        dma((parts, len(groups))),
     ]
-    shape = jax.ShapeDtypeStruct((modes, rows, cells), f32)
+    shape = pltpu.VMEM((modes, rows, cells), f32)
     return pl.pallas_call(
         functools.partial(kernel, tiles, levs, groups, rows, modes, cells, levels),
         out_shape=(shape, shape),
         in_specs=[pl.BlockSpec(memory_space=pl.ANY), pl.BlockSpec(memory_space=pltpu.VMEM),
                   pl.BlockSpec(memory_space=pltpu.VMEM)],
-        out_specs=(pl.BlockSpec(memory_space=pl.ANY), pl.BlockSpec(memory_space=pl.ANY)),
+        out_specs=(pl.BlockSpec(memory_space=pltpu.VMEM), pl.BlockSpec(memory_space=pltpu.VMEM)),
         scratch_shapes=scratch,
-        compiler_params=pltpu.CompilerParams(collective_id=0, has_side_effects=True, vmem_limit_bytes=67000000),
-    )(increments.reshape(own_levels * rows, cells), projection, helmholtz.reshape(1, modes))
+        compiler_params=pltpu.CompilerParams(collective_id=0, has_side_effects=True, vmem_limit_bytes=52000000),
+    )(increments.reshape(own_levels * rows, cells), projection.T, helmholtz.reshape(1, modes))
 
 
 def solution(mesh):

time: 88.9 us -> 56.9 us (0.64)
  Pallas kernels: 81.3 us -> 53.1 us
  local copies, waits for them, and re-layouts: 6.68 us -> 2.99 us
    pallas_call x1, Pallas kernels: 81.3 us -> 53.1 us  [shards(): pl.pallas_call(functools.partial(kernel, tiles, levs, groups, rows, modes...]
    unnamed x5 -> x2, local copies, waits for them, and re-layouts: 6.68 us -> 2.99 us
where the time goes in v2:
time: 56.9 us; the launch traced here: 56.8 us
  Pallas kernels  53.1 us (93%)
  local copies, waits for them, and re-layouts  2.99 us (5%)
  between operations  0.64 us (1%)
    pallas_call x1, Pallas kernels, shards(): pl.pallas_call(functools.partial(kernel, tiles, levs, groups, rows, modes...  53.1 us
    unnamed x2, local copies, waits for them, and re-layouts  2.99 us

profile of v2, /device:TPU:0, one launch (start us, length us, event | category | flops | bytes accessed | tf_op | source)
XLA Modules:
  0.0 56.8 jit_solution(13271248209176424856)
XLA Ops:
  0.6 53.1 %shard_map.50 = (f32[40,16,1024]{2,1,0:T(8,128)S(1)}, f32[40,16,1024]{2,1,0:T(8,128)S(1)}) custom-call(bf16[1088,1024]{1,0:T(8,128)(2,1)} %bitcast.3, bf16[136,80]{1,0:T(8,128)(2,1)} %bitcast.4, f32[1,40]{1,0:T(1,128)} %bitcast.5), custom_call_target="tpu_custom_call" | custom-call | tf_op jit(solution)/shard_map/pallas_call | solution.py:454
  53.8 1.5 %copy.7 = f32[40,16,1024]{2,1,0:T(8,128)} copy(f32[40,16,1024]{2,1,0:T(8,128)S(1)} %get-tuple-element.2) | data formatting | bytes 5242880
  55.3 1.5 %copy.8 = f32[40,16,1024]{2,1,0:T(8,128)} copy(f32[40,16,1024]{2,1,0:T(8,128)S(1)} %get-tuple-element.3) | data formatting | bytes 5242880

commit v3 on v2

--- a/solution.py
+++ b/solution.py
@@ -12,8 +12,6 @@
 HALF = HALO // 2
 POWER = 13
 SUB = 8
-RING = 3
-LAG = 2
 LANE = 128
 CHUNKS = 4
 MESH = pl.DeviceIdType.MESH
@@ -28,6 +26,17 @@
         groups.append(size)
         count //= size
     return groups
+
+
+def reaches(tiles):
+    return [2 ** r for r in range(tiles.bit_length()) if 2 ** r < tiles - 1]
+
+
+def starts(rows):
+    places = [0]
+    for k in range(1, STEPS + 1):
+        places.append(places[-1] + rows + 2 * (HALO - k))
+    return places
 
 
 def encode(value, scale):
@@ -96,8 +105,8 @@
 
 
 def kernel(tiles, levs, groups, rows, modes, cells, levels, inc_ref, proj_ref, helm_ref, sol_ref, res_ref,
-           x_all, wide, base, powers, out_buf, in_buf, thetas, sums, grams,
-           local_sem, swap_send, swap_recv, halo_send, halo_recv, gram_send, gram_recv):
+           x_all, wide, base, powers, out_buf, in_buf, thetas, sums, grams, proj_own, helm_own,
+           local_sem, small_sems, known, swap_send, swap_recv, halo_send, halo_recv, gram_send, gram_recv):
     tile = lax.axis_index("tile")
     lev = lax.axis_index("lev")
     part = inc_ref.shape[0]
@@ -117,20 +126,43 @@
     for j in range(1, levs):
         pl.semaphore_signal(barrier, 1, device_id=(tile, lax.rem(lev + j, levs)), device_id_type=MESH)
         count += 1
-    for peer in (lax.rem(tile + 1, tiles), lax.rem(tile + tiles - 1, tiles)):
-        pl.semaphore_signal(barrier, 1, device_id=(peer, lev), device_id_type=MESH)
-        count += 1
-    for digit, peers in stage_peers:
-        for peer in peers:
+    def toward(distance):
+        return [(lax.max(tile - distance, 0), tile >= distance),
+                (lax.min(tile + distance, tiles - 1), tile < tiles - distance)]
+
+    for peer, there in toward(1):
+        @pl.when(there)
+        def _(peer=peer):
             pl.semaphore_signal(barrier, 1, device_id=(peer, lev), device_id_type=MESH)
-            count += 1
-
+        count += jnp.where(there, 1, 0)
     local = pltpu.make_async_copy(inc_ref, x_all.at[0], local_sem)
+    small = [pltpu.make_async_copy(proj_ref, proj_own, small_sems.at[0]),
+             pltpu.make_async_copy(helm_ref, helm_own, small_sems.at[1])]
+    for copy in small:
+        copy.start()
     local.start()
 
     chunk = cells // CHUNKS
     with jax.named_scope("barrier"):
         pl.semaphore_wait(barrier, count)
+
+    rounds = reaches(tiles)
+
+    def greet(r):
+        if r < len(rounds):
+            for way, (peer, there) in enumerate(toward(rounds[r])):
+                @pl.when(there)
+                def _(way=way, peer=peer):
+                    pl.semaphore_signal(known.at[r, way], 1, device_id=(peer, lev), device_id_type=MESH)
+
+    def greeted(r):
+        if r < len(rounds):
+            for way, (peer, there) in enumerate(toward(rounds[r])):
+                @pl.when(there)
+                def _(way=way):
+                    pl.semaphore_wait(known.at[r, 1 - way], 1)
+
+    greet(0)
 
     def swap(j, c):
         cols = pl.ds(c * chunk, chunk)
@@ -142,7 +174,9 @@
         for j in range(1, levs):
             swap(j, c).start()
 
-    proj = proj_ref[...].astype(f32)
+    for copy in small:
+        copy.wait()
+    proj = proj_own[...].astype(f32)
     own = proj[:, 0:modes]
     for j in range(1, levs):
         own = jnp.where(lev == j, proj[:, j * modes:(j + 1) * modes], own)
@@ -184,9 +218,11 @@
     with jax.named_scope("widen"):
         for j in range(1, levs):
             widen(j)
+    greeted(0)
+    greet(1)
 
     diag = lax.broadcasted_iota(jnp.int32, (modes, modes), 0) == lax.broadcasted_iota(jnp.int32, (modes, modes), 1)
-    helm = jnp.sum(jnp.where(diag, jnp.broadcast_to(helm_ref[...], (modes, modes)), 0.0), axis=1, keepdims=True)
+    helm = jnp.sum(jnp.where(diag, jnp.broadcast_to(helm_own[...], (modes, modes)), 0.0), axis=1, keepdims=True)
     thetas[...] = jnp.broadcast_to(4.0 / (4.0 + helm), (modes, LANE))
     has = {0: tile < tiles - 1, 1: tile > 0}
     for side in range(2):
@@ -237,11 +273,14 @@
     with jax.named_scope("other"):
         for c in range(CHUNKS):
             for j in range(1, levs):
-                swap(j, c).wait_recv()
+                with jax.named_scope("arrive"):
+                    swap(j, c).wait_recv()
                 project(j, c)
             send_chunk(c)
-    if parts > 1:
-        send(1)
+    greeted(1)
+    greet(2)
+    for g in range(1, parts):
+        send(g)
 
     lane = lax.broadcasted_iota(jnp.int32, (SUB, LANE), 1)
     first_lane = lane == 0
@@ -268,18 +307,19 @@
     inside = jnp.float32(0.5)
     factor = {0: jnp.where(tile > 0, inside, 0.0), 1: jnp.where(tile < tiles - 1, inside, 0.0)}
 
-    def field(g, k):
-        return base.at[g] if k == 0 else powers.at[lax.rem(g, RING), k - 1]
+    places = starts(rows)
+
+    def field(g, k, row):
+        if k == 0:
+            return base.at[g, row + HALO]
+        return powers.at[g, places[k - 1] + row + HALO - k]
 
     def extend(g, k, ranges):
-        src, dst = field(g, k - 1), field(g, k)
-        before = field(g, k - 2) if k > 1 else None
         totals = {}
         for low, high in ranges:
             for row in range(low, high):
-                at = row + HALO
-                here = src[at]
-                around = src[at - 1] + src[at + 1] + beside(here)
+                here = field(g, k - 1, row)[...]
+                around = field(g, k - 1, row - 1)[...] + field(g, k - 1, row + 1)[...] + beside(here)
                 if row < 0:
                     gain = factor[0]
                 elif row >= rows:
@@ -289,9 +329,9 @@
                 if k == 1:
                     gain = gain * 0.5
                 fresh = gain * around
-                if before is not None:
-                    fresh = fresh - before[at]
-                dst[at] = fresh
+                if k > 1:
+                    fresh = fresh - field(g, k - 2, row)[...]
+                field(g, k, row)[...] = fresh
                 if 0 <= row < rows:
                     if k == 1:
                         totals[0] = add(totals.get(0), fold(here * here))
@@ -299,7 +339,7 @@
                     if k < STEPS:
                         totals[2 * k] = add(totals.get(2 * k), fold(fresh * fresh))
         for slot, value in totals.items():
-            sums[slot] = sums[slot] + value
+            sums[g, slot] = sums[g, slot] + value
 
     def interior(g):
         with jax.named_scope("interior"):
@@ -328,6 +368,7 @@
                 extend(g, k, [(k - new, k - old), (rows - k + old, rows - k + new)])
 
     products = 2 * STEPS
+    offset = lane - products * lax.broadcasted_iota(jnp.int32, (SUB, LANE), 0)
 
     def modes_of(g):
         return pl.ds(pl.multiple_of(g * SUB, SUB), SUB)
@@ -354,11 +395,10 @@
 
     def total(g):
         with jax.named_scope("total"):
-            lanes = lax.broadcasted_iota(jnp.int32, (SUB, LANE), 1)
             table = jnp.zeros((SUB, LANE), f32)
             for slot in range(products):
-                table = jnp.where(lanes == slot, jnp.sum(sums[slot], axis=1, keepdims=True), table)
-            sums[...] = jnp.zeros_like(sums)
+                table = jnp.where(offset == slot, jnp.sum(sums[g, slot], axis=1, keepdims=True), table)
+            table = jnp.sum(table, axis=0, keepdims=True)
             gram_start(g, 0, table)
 
     def finish(g):
@@ -368,17 +408,20 @@
                 if stage + 1 < len(groups):
                     gram_start(g, stage + 1, table)
         with jax.named_scope("coef"):
-            columns = [jnp.broadcast_to(table[:, slot:slot + 1], (SUB, LANE)) for slot in range(products)]
+            table = jnp.broadcast_to(table, (SUB, LANE))
+            columns = []
+            for slot in range(products):
+                column = jnp.sum(jnp.where(offset == slot, table, 0.0), axis=1, keepdims=True)
+                columns.append(jnp.broadcast_to(column, (SUB, LANE)))
             x, r = coefficients(columns, thetas[modes_of(g)])
         with jax.named_scope("combine"):
             for row in range(rows):
-                at = row + HALO
                 solved, left = [], []
                 for j in range(across):
                     cols = slice(j * LANE, (j + 1) * LANE)
                     x_sum = r_sum = None
                     for k in range(STEPS + 1):
-                        value = field(g, k)[at, :, cols]
+                        value = field(g, k, row)[:, cols]
                         r_sum = add(r_sum, r[k] * value)
                         if k < STEPS:
                             x_sum = add(x_sum, x[k] * value)
@@ -389,26 +432,25 @@
 
     sums[...] = jnp.zeros_like(sums)
 
-    def advance(index, carry):
-        @pl.when(index < parts)
-        def _():
-            interior(index)
-            for half in range(2):
-                take(index, half)
-                outer(index, half)
-            total(index)
-
-        @pl.when(index + LAG < parts)
-        def _():
-            send(index + LAG)
-
-        @pl.when(index >= LAG)
-        def _():
-            finish(index - LAG)
-
-        return carry
-
-    lax.fori_loop(0, parts + LAG, advance, 0)
+    def each(body):
+        def step(index, carry):
+            body(index)
+            return carry
+
+        lax.fori_loop(0, parts, step, 0)
+
+    def gather(g):
+        for half in range(2):
+            take(g, half)
+            outer(g, half)
+        total(g)
+
+    each(interior)
+    for r in range(2, len(rounds)):
+        greeted(r)
+        greet(r + 1)
+    each(gather)
+    each(finish)
 
     with jax.named_scope("drain"):
         for j in range(1, levs):
@@ -436,13 +478,17 @@
         vmem((levs, own_levels * rows, cells), bf16),
         vmem((levs, rows * modes, own_levels * rows), bf16),
         vmem((parts, rows + 2 * HALO, SUB, cells), f32),
-        vmem((RING, STEPS, rows + 2 * HALO, SUB, cells), f32),
+        vmem((parts, starts(rows)[-1], SUB, cells), f32),
         vmem((parts, 2, 2, HALF * SUB, cells), bf16),
         vmem((parts, 2, 2, HALF * SUB, cells), bf16),
         vmem((modes, LANE), f32),
-        vmem((2 * STEPS, SUB, LANE), f32),
-        vmem((parts, len(groups), most, SUB, LANE), f32),
+        vmem((parts, 2 * STEPS, SUB, LANE), f32),
+        vmem((parts, len(groups), most, 1, LANE), f32),
+        vmem((levels, levs * modes), bf16),
+        vmem((1, modes), f32),
         dma,
+        dma((2,)),
+        pltpu.SemaphoreType.REGULAR((len(reaches(tiles)) + 1, 2)),
         dma((levs - 1, CHUNKS)),
         dma((levs - 1, CHUNKS)),
         dma((parts, 2, 2)),
@@ -454,8 +500,7 @@
     return pl.pallas_call(
         functools.partial(kernel, tiles, levs, groups, rows, modes, cells, levels),
         out_shape=(shape, shape),
-        in_specs=[pl.BlockSpec(memory_space=pl.ANY), pl.BlockSpec(memory_space=pltpu.VMEM),
-                  pl.BlockSpec(memory_space=pltpu.VMEM)],
+        in_specs=[pl.BlockSpec(memory_space=pl.ANY)] * 3,
         out_specs=(pl.BlockSpec(memory_space=pltpu.VMEM), pl.BlockSpec(memory_space=pltpu.VMEM)),
         scratch_shapes=scratch,
         compiler_params=pltpu.CompilerParams(collective_id=0, has_side_effects=True, vmem_limit_bytes=52000000),

time: 56.9 us -> 50.3 us (0.88)
  Pallas kernels: 53.1 us -> 46.5 us
    pallas_call x1, Pallas kernels: 53.1 us -> 46.5 us  [shards(): pl.pallas_call(functools.partial(kernel, tiles, levs, groups, rows, modes...]
where the time goes in v3:
time: 50.3 us; the launch traced here: 50.1 us
  Pallas kernels  46.5 us (92%)
  local copies, waits for them, and re-layouts  2.99 us (6%)
  between operations  0.64 us (1%)
    pallas_call x1, Pallas kernels, shards(): pl.pallas_call(functools.partial(kernel, tiles, levs, groups, rows, modes...  46.5 us
    unnamed x2, local copies, waits for them, and re-layouts  2.99 us

profile of v3, /device:TPU:0, one launch (start us, length us, event | category | flops | bytes accessed | tf_op | source)
XLA Modules:
  0.0 50.1 jit_solution(4321360424924174788)
XLA Ops:
  0.6 46.5 %shard_map.50 = (f32[40,16,1024]{2,1,0:T(8,128)S(1)}, f32[40,16,1024]{2,1,0:T(8,128)S(1)}) custom-call(bf16[1088,1024]{1,0:T(8,128)(2,1)} %bitcast.3, bf16[136,80]{1,0:T(8,128)(2,1)} %bitcast.4, f32[1,40]{1,0:T(1,128)} %bitcast.5), custom_call_target="tpu_custom_call" | custom-call | tf_op jit(solution)/shard_map/pallas_call | solution.py:500
  47.1 1.5 %copy.7 = f32[40,16,1024]{2,1,0:T(8,128)} copy(f32[40,16,1024]{2,1,0:T(8,128)S(1)} %get-tuple-element.2) | data formatting | bytes 5242880
  48.6 1.5 %copy.8 = f32[40,16,1024]{2,1,0:T(8,128)} copy(f32[40,16,1024]{2,1,0:T(8,128)S(1)} %get-tuple-element.3) | data formatting | bytes 5242880

commit v4 on v3

--- a/solution.py
+++ b/solution.py
@@ -104,6 +104,14 @@
     return x, r
 
 
+def write(sol_in, res_in, sol_ref, res_ref, sems):
+    copies = [pltpu.make_async_copy(sol_in, sol_ref, sems.at[0]), pltpu.make_async_copy(res_in, res_ref, sems.at[1])]
+    for copy in copies:
+        copy.start()
+    for copy in copies:
+        copy.wait()
+
+
 def kernel(tiles, levs, groups, rows, modes, cells, levels, inc_ref, proj_ref, helm_ref, sol_ref, res_ref,
            x_all, wide, base, powers, out_buf, in_buf, thetas, sums, grams, proj_own, helm_own,
            local_sem, small_sems, known, swap_send, swap_recv, halo_send, halo_recv, gram_send, gram_recv):
@@ -185,36 +193,38 @@
     col_e = lax.broadcasted_iota(jnp.int32, (own_levels, part), 1)
     row_e = lax.broadcasted_iota(jnp.int32, (own_levels, part), 0) * rows
     onehot = jnp.where((col_e >= row_e) & (col_e < row_e + rows), 1.0, 0.0).astype(bf16)
-    col_w = lax.rem(lax.broadcasted_iota(jnp.int32, (2 * modes, part), 1), rows)
-    second = jnp.where(lax.broadcasted_iota(jnp.int32, (2 * modes, part), 0) >= modes, 1, 0)
-    pick = col_w - second
+    block = rows * SUB
+    mask = lax.rem(lax.broadcasted_iota(jnp.int32, (block, part), 1), rows) == lax.div(
+        lax.broadcasted_iota(jnp.int32, (block, part), 0), SUB)
 
     def widen(position):
         chosen = groups_l[position]
         for j in range(1, levs):
             chosen = jnp.where(lev == j, groups_l[(j + position) % levs], chosen)
-        twice = jnp.concatenate([chosen, chosen], axis=1).astype(bf16)
-        repeated = lax.dot_general(twice, onehot, (((0,), (0,)), ((), ())), preferred_element_type=f32)
-        for pair in range(rows // 2):
-            wide[position, pair * 2 * modes:(pair + 1) * 2 * modes, :] = jnp.where(
-                pick == 2 * pair, repeated, 0.0).astype(bf16)
-
-    def project(position, c):
+        repeated = lax.dot_general(
+            chosen.astype(bf16), onehot, (((0,), (0,)), ((), ())), preferred_element_type=f32)
+        for g in range(parts):
+            tall = jnp.concatenate([repeated[g * SUB:(g + 1) * SUB]] * rows, axis=0)
+            wide[position, g * block:(g + 1) * block, :] = jnp.where(mask, tall, 0.0).astype(bf16)
+
+    def project(positions, c, first, number, adding=False):
         cols = slice(c * chunk, (c + 1) * chunk)
-        got = jnp.dot(wide[position], x_all[position, :, cols], preferred_element_type=f32)
-        got = got.reshape(rows, parts, SUB, chunk)
-        for g in range(parts):
-            value = got[:, g]
-            if position:
-                value = base[g, HALO:HALO + rows, :, cols] + value
-            base[g, HALO:HALO + rows, :, cols] = value
+        got = None
+        for position in positions:
+            got = add(got, jnp.dot(wide[position, first * block:(first + number) * block], x_all[position, :, cols],
+                                   preferred_element_type=f32))
+        for g in range(number):
+            value = got[g * block:(g + 1) * block].reshape(rows, SUB, chunk)
+            if adding:
+                value = base[first + g, HALO:HALO + rows, :, cols] + value
+            base[first + g, HALO:HALO + rows, :, cols] = value
 
     with jax.named_scope("widen"):
         widen(0)
     with jax.named_scope("own"):
         local.wait()
         for c in range(CHUNKS):
-            project(0, c)
+            project([0], c, 0, 1)
     with jax.named_scope("widen"):
         for j in range(1, levs):
             widen(j)
@@ -250,15 +260,15 @@
         width = cols.stop - cols.start
         out_buf[g, side, half, :, cols] = encode(base[g, first:first + HALF, :, cols].reshape(HALF * SUB, width), scale)
 
-    def send_chunk(c):
+    def send_chunk(g, c):
         cols = pl.ds(c * chunk, chunk)
         for half in range(2):
             for side in range(2):
-                encode_part(0, half, side, slice(c * chunk, (c + 1) * chunk))
+                encode_part(g, half, side, slice(c * chunk, (c + 1) * chunk))
 
                 @pl.when(sends[side])
                 def _(half=half, side=side):
-                    halo_copy(0, side, half, cols).start()
+                    halo_copy(g, side, half, cols).start()
 
     def send(g):
         with jax.named_scope("send"):
@@ -272,14 +282,20 @@
 
     with jax.named_scope("other"):
         for c in range(CHUNKS):
-            for j in range(1, levs):
-                with jax.named_scope("arrive"):
+            with jax.named_scope("arrive"):
+                for j in range(1, levs):
                     swap(j, c).wait_recv()
-                project(j, c)
-            send_chunk(c)
+            project(range(1, levs), c, 0, 1, True)
+            send_chunk(0, c)
     greeted(1)
     greet(2)
-    for g in range(1, parts):
+    with jax.named_scope("rest"):
+        for c in range(CHUNKS):
+            for g in range(1, parts, 2):
+                project(range(levs), c, g, min(2, parts - g))
+            if parts > 1:
+                send_chunk(1, c)
+    for g in range(2, parts):
         send(g)
 
     lane = lax.broadcasted_iota(jnp.int32, (SUB, LANE), 1)
@@ -347,25 +363,24 @@
                 if rows - k > k:
                     extend(g, k, [(k, rows - k)])
 
-    def take(g, half):
+    def take(g, half, side):
         with jax.named_scope("take"):
-            for side in range(2):
-                @pl.when(has[side])
-                def _(side=side):
-                    halo_copy(g, side, half).wait_recv()
+            @pl.when(has[side])
+            def _():
+                halo_copy(g, side, half).wait_recv()
         with jax.named_scope("decode"):
-            for side in range(2):
-                if side == 0:
-                    first = HALO + rows + half * HALF
-                else:
-                    first = HALO - (half + 1) * HALF
-                base[g, first:first + HALF] = decode(in_buf[g, side, half], scale).reshape(HALF, SUB, cells)
-
-    def outer(g, half):
+            if side == 0:
+                first = HALO + rows + half * HALF
+            else:
+                first = HALO - (half + 1) * HALF
+            base[g, first:first + HALF] = decode(in_buf[g, side, half], scale).reshape(HALF, SUB, cells)
+
+    def outer(g, half, sides):
         with jax.named_scope("outer"):
             old, new = half * HALF, (half + 1) * HALF
             for k in range(1, STEPS + 1):
-                extend(g, k, [(k - new, k - old), (rows - k + old, rows - k + new)])
+                ranges = {0: (rows - k + old, rows - k + new), 1: (k - new, k - old)}
+                extend(g, k, [ranges[side] for side in sides])
 
     products = 2 * STEPS
     offset = lane - products * lax.broadcasted_iota(jnp.int32, (SUB, LANE), 0)
@@ -441,8 +456,9 @@
 
     def gather(g):
         for half in range(2):
-            take(g, half)
-            outer(g, half)
+            for side in range(2):
+                take(g, half, side)
+            outer(g, half, (1, 0))
         total(g)
 
     each(interior)
@@ -497,7 +513,7 @@
         dma((parts, len(groups))),
     ]
     shape = pltpu.VMEM((modes, rows, cells), f32)
-    return pl.pallas_call(
+    kept = pl.pallas_call(
         functools.partial(kernel, tiles, levs, groups, rows, modes, cells, levels),
         out_shape=(shape, shape),
         in_specs=[pl.BlockSpec(memory_space=pl.ANY)] * 3,
@@ -505,6 +521,13 @@
         scratch_shapes=scratch,
         compiler_params=pltpu.CompilerParams(collective_id=0, has_side_effects=True, vmem_limit_bytes=52000000),
     )(increments.reshape(own_levels * rows, cells), projection.T, helmholtz.reshape(1, modes))
+    outside = pl.BlockSpec(memory_space=pl.ANY)
+    inside = pl.BlockSpec(memory_space=vmem)
+    shape = jax.ShapeDtypeStruct((modes, rows, cells), f32)
+    return pl.pallas_call(
+        write, out_shape=(shape, shape), in_specs=[inside] * 2, out_specs=(outside, outside),
+        scratch_shapes=[dma((2,))], compiler_params=pltpu.CompilerParams(vmem_limit_bytes=1000000),
+    )(*kept)
 
 
 def solution(mesh):

time: 50.3 us -> 48.5 us (0.964)
  local copies, waits for them, and re-layouts: 2.99 us -> 0 us
  Pallas kernels: 46.5 us -> 47.7 us
    unnamed x2 -> x0, local copies, waits for them, and re-layouts: 2.99 us -> none
    pallas_call x0 -> x1, Pallas kernels: none -> 2.37 us  [shards(): pl.pallas_call(write, out_shape=(shape, shape), in_specs=[inside] * 2, ou...]
    pallas_call x1, Pallas kernels: 46.5 us -> 45.3 us  [shards(): pl.pallas_call(functools.partial(kernel, tiles, levs, groups, rows, modes...]
where the time goes in v4:
time: 48.5 us; the launch traced here: 48.3 us
  Pallas kernels  47.7 us (98%)
  between operations  0.64 us (1%)
    pallas_call x1, Pallas kernels, shards(): pl.pallas_call(functools.partial(kernel, tiles, levs, groups, rows, modes...  45.3 us
    pallas_call x1, Pallas kernels, shards(): pl.pallas_call(write, out_shape=(shape, shape), in_specs=[inside] * 2, ou...  2.37 us

profile of v4, /device:TPU:0, one launch (start us, length us, event | category | flops | bytes accessed | tf_op | source)
XLA Modules:
  0.0 48.3 jit_solution(10414562757788210093)
XLA Ops:
  0.6 45.3 %shard_map.50 = (f32[40,16,1024]{2,1,0:T(8,128)S(1)}, f32[40,16,1024]{2,1,0:T(8,128)S(1)}) custom-call(bf16[1088,1024]{1,0:T(8,128)(2,1)} %bitcast.3, bf16[136,80]{1,0:T(8,128)(2,1)} %bitcast.4, f32[1,40]{1,0:T(1,128)} %bitcast.5), custom_call_target="tpu_custom_call" | custom-call | tf_op jit(solution)/shard_map/pallas_call | solution.py:516
  46.0 2.4 %shard_map.51 = (f32[40,16,1024]{2,1,0:T(8,128)}, f32[40,16,1024]{2,1,0:T(8,128)}) custom-call(f32[40,16,1024]{2,1,0:T(8,128)S(1)} %get-tuple-element.4.sol_in, f32[40,16,1024]{2,1,0:T(8,128)S(1)} %get-tuple-element.5.res_in), custom_call_target="tpu_custom_call" | custom-call | tf_op jit(solution)/shard_map/pallas_call | solution.py:527

commit v5 on v4

--- a/solution.py
+++ b/solution.py
@@ -13,7 +13,8 @@
 POWER = 13
 SUB = 8
 LANE = 128
-CHUNKS = 4
+CHUNKS = 8
+WIDER = 2
 MESH = pl.DeviceIdType.MESH
 f32 = jnp.float32
 bf16 = jnp.bfloat16
@@ -104,16 +105,47 @@
     return x, r
 
 
-def write(sol_in, res_in, sol_ref, res_ref, sems):
-    copies = [pltpu.make_async_copy(sol_in, sol_ref, sems.at[0]), pltpu.make_async_copy(res_in, res_ref, sems.at[1])]
-    for copy in copies:
+def combine(first, powers, x, r, solved, left):
+    rows, cells = solved.shape[1:]
+    places = starts(rows)
+    for row in range(rows):
+        for j in range(cells // LANE):
+            cols = slice(j * LANE, (j + 1) * LANE)
+            x_sum = r_sum = None
+            for k in range(STEPS + 1):
+                if k == 0:
+                    value = first[row + HALO, :, cols]
+                else:
+                    value = powers[places[k - 1] + row + HALO - k, :, cols]
+                r_sum = add(r_sum, r[k] * value)
+                if k < STEPS:
+                    x_sum = add(x_sum, x[k] * value)
+            solved[:, row, cols] = x_sum
+            left[:, row, cols] = r_sum
+
+
+def write(parts, sol_in, res_in, base, tail, last, sol_ref, res_ref, ready, sems):
+    done = (parts - 1) * SUB
+    copies = []
+
+    def put(src, dst):
+        copy = pltpu.make_async_copy(src, dst, sems.at[len(copies)])
         copy.start()
+        copies.append(copy)
+
+    if done:
+        put(sol_in, sol_ref.at[pl.ds(0, done)])
+        put(res_in, res_ref.at[pl.ds(0, done)])
+    coefs = [last[k] for k in range(2 * STEPS + 1)]
+    combine(base.at[parts - 1], tail, coefs[:STEPS], coefs[STEPS:], ready.at[0], ready.at[1])
+    put(ready.at[0], sol_ref.at[pl.ds(done, SUB)])
+    put(ready.at[1], res_ref.at[pl.ds(done, SUB)])
     for copy in copies:
         copy.wait()
 
 
-def kernel(tiles, levs, groups, rows, modes, cells, levels, inc_ref, proj_ref, helm_ref, sol_ref, res_ref,
-           x_all, wide, base, powers, out_buf, in_buf, thetas, sums, grams, proj_own, helm_own,
+def kernel(tiles, levs, groups, rows, modes, cells, levels, inc_ref, proj_ref, helm_ref, sol_ref, res_ref, base, tail, last,
+           x_all, wide, powers, out_buf, in_buf, thetas, sums, grams, proj_own, helm_own,
            local_sem, small_sems, known, swap_send, swap_recv, halo_send, halo_recv, gram_send, gram_recv):
     tile = lax.axis_index("tile")
     lev = lax.axis_index("lev")
@@ -207,14 +239,14 @@
             tall = jnp.concatenate([repeated[g * SUB:(g + 1) * SUB]] * rows, axis=0)
             wide[position, g * block:(g + 1) * block, :] = jnp.where(mask, tall, 0.0).astype(bf16)
 
-    def project(positions, c, first, number, adding=False):
-        cols = slice(c * chunk, (c + 1) * chunk)
+    def project(positions, c, first, number, adding=False, wide_by=1):
+        cols = slice(c * chunk, (c + wide_by) * chunk)
         got = None
         for position in positions:
             got = add(got, jnp.dot(wide[position, first * block:(first + number) * block], x_all[position, :, cols],
                                    preferred_element_type=f32))
         for g in range(number):
-            value = got[g * block:(g + 1) * block].reshape(rows, SUB, chunk)
+            value = got[g * block:(g + 1) * block].reshape(rows, SUB, wide_by * chunk)
             if adding:
                 value = base[first + g, HALO:HALO + rows, :, cols] + value
             base[first + g, HALO:HALO + rows, :, cols] = value
@@ -223,8 +255,8 @@
         widen(0)
     with jax.named_scope("own"):
         local.wait()
-        for c in range(CHUNKS):
-            project([0], c, 0, 1)
+        for c in range(0, CHUNKS, WIDER):
+            project([0], c, 0, 1, wide_by=WIDER)
     with jax.named_scope("widen"):
         for j in range(1, levs):
             widen(j)
@@ -260,11 +292,11 @@
         width = cols.stop - cols.start
         out_buf[g, side, half, :, cols] = encode(base[g, first:first + HALF, :, cols].reshape(HALF * SUB, width), scale)
 
-    def send_chunk(g, c):
-        cols = pl.ds(c * chunk, chunk)
+    def send_chunk(g, c, wide_by=1):
+        cols = pl.ds(c * chunk, wide_by * chunk)
         for half in range(2):
             for side in range(2):
-                encode_part(g, half, side, slice(c * chunk, (c + 1) * chunk))
+                encode_part(g, half, side, slice(c * chunk, (c + wide_by) * chunk))
 
                 @pl.when(sends[side])
                 def _(half=half, side=side):
@@ -290,11 +322,11 @@
     greeted(1)
     greet(2)
     with jax.named_scope("rest"):
-        for c in range(CHUNKS):
+        for c in range(0, CHUNKS, WIDER):
             for g in range(1, parts, 2):
-                project(range(levs), c, g, min(2, parts - g))
+                project(range(levs), c, g, min(2, parts - g), wide_by=WIDER)
             if parts > 1:
-                send_chunk(1, c)
+                send_chunk(1, c, WIDER)
     for g in range(2, parts):
         send(g)
 
@@ -328,7 +360,10 @@
     def field(g, k, row):
         if k == 0:
             return base.at[g, row + HALO]
-        return powers.at[g, places[k - 1] + row + HALO - k]
+        at = places[k - 1] + row + HALO - k
+        if isinstance(g, int) and g == parts - 1:
+            return tail.at[at]
+        return powers.at[g, at]
 
     def extend(g, k, ranges):
         totals = {}
@@ -416,7 +451,7 @@
             table = jnp.sum(table, axis=0, keepdims=True)
             gram_start(g, 0, table)
 
-    def finish(g):
+    def solve(g):
         with jax.named_scope("gram"):
             for stage in range(len(groups)):
                 table = gram_finish(g, stage)
@@ -428,31 +463,21 @@
             for slot in range(products):
                 column = jnp.sum(jnp.where(offset == slot, table, 0.0), axis=1, keepdims=True)
                 columns.append(jnp.broadcast_to(column, (SUB, LANE)))
-            x, r = coefficients(columns, thetas[modes_of(g)])
+            return coefficients(columns, thetas[modes_of(g)])
+
+    def finish(g):
+        x, r = solve(g)
         with jax.named_scope("combine"):
-            for row in range(rows):
-                solved, left = [], []
-                for j in range(across):
-                    cols = slice(j * LANE, (j + 1) * LANE)
-                    x_sum = r_sum = None
-                    for k in range(STEPS + 1):
-                        value = field(g, k, row)[:, cols]
-                        r_sum = add(r_sum, r[k] * value)
-                        if k < STEPS:
-                            x_sum = add(x_sum, x[k] * value)
-                    solved.append(x_sum)
-                    left.append(r_sum)
-                sol_ref[modes_of(g), row, :] = jnp.concatenate(solved, axis=1)
-                res_ref[modes_of(g), row, :] = jnp.concatenate(left, axis=1)
+            combine(base.at[g], powers.at[g], x, r, sol_ref.at[modes_of(g)], res_ref.at[modes_of(g)])
 
     sums[...] = jnp.zeros_like(sums)
 
-    def each(body):
+    def each(body, number=parts, start=0):
         def step(index, carry):
             body(index)
             return carry
 
-        lax.fori_loop(0, parts, step, 0)
+        lax.fori_loop(start, number, step, 0)
 
     def gather(g):
         for half in range(2):
@@ -461,12 +486,17 @@
             outer(g, half, (1, 0))
         total(g)
 
-    each(interior)
+    each(interior, parts - 1)
+    interior(parts - 1)
     for r in range(2, len(rounds)):
         greeted(r)
         greet(r + 1)
-    each(gather)
-    each(finish)
+    each(gather, parts - 1)
+    gather(parts - 1)
+    each(finish, parts - 1)
+    x, r = solve(parts - 1)
+    for k, value in enumerate(x + r):
+        last[k] = value
 
     with jax.named_scope("drain"):
         for j in range(1, levs):
@@ -493,8 +523,7 @@
     scratch = [
         vmem((levs, own_levels * rows, cells), bf16),
         vmem((levs, rows * modes, own_levels * rows), bf16),
-        vmem((parts, rows + 2 * HALO, SUB, cells), f32),
-        vmem((parts, starts(rows)[-1], SUB, cells), f32),
+        vmem((max(parts - 1, 1), starts(rows)[-1], SUB, cells), f32),
         vmem((parts, 2, 2, HALF * SUB, cells), bf16),
         vmem((parts, 2, 2, HALF * SUB, cells), bf16),
         vmem((modes, LANE), f32),
@@ -512,21 +541,27 @@
         dma((parts, len(groups))),
         dma((parts, len(groups))),
     ]
-    shape = pltpu.VMEM((modes, rows, cells), f32)
+    shape = vmem((max(parts - 1, 1) * SUB, rows, cells), f32)
+    held = (shape, shape, vmem((parts, rows + 2 * HALO, SUB, cells), f32),
+            vmem((starts(rows)[-1], SUB, cells), f32), vmem((2 * STEPS + 1, SUB, LANE), f32))
+    inside = pl.BlockSpec(memory_space=vmem)
+    outside = pl.BlockSpec(memory_space=pl.ANY)
     kept = pl.pallas_call(
         functools.partial(kernel, tiles, levs, groups, rows, modes, cells, levels),
-        out_shape=(shape, shape),
-        in_specs=[pl.BlockSpec(memory_space=pl.ANY)] * 3,
-        out_specs=(pl.BlockSpec(memory_space=pltpu.VMEM), pl.BlockSpec(memory_space=pltpu.VMEM)),
+        out_shape=held,
+        in_specs=[outside] * 3,
+        out_specs=(inside,) * len(held),
         scratch_shapes=scratch,
-        compiler_params=pltpu.CompilerParams(collective_id=0, has_side_effects=True, vmem_limit_bytes=52000000),
+        compiler_params=pltpu.CompilerParams(collective_id=0, has_side_effects=True, vmem_limit_bytes=50000000),
     )(increments.reshape(own_levels * rows, cells), projection.T, helmholtz.reshape(1, modes))
-    outside = pl.BlockSpec(memory_space=pl.ANY)
-    inside = pl.BlockSpec(memory_space=vmem)
     shape = jax.ShapeDtypeStruct((modes, rows, cells), f32)
     return pl.pallas_call(
-        write, out_shape=(shape, shape), in_specs=[inside] * 2, out_specs=(outside, outside),
-        scratch_shapes=[dma((2,))], compiler_params=pltpu.CompilerParams(vmem_limit_bytes=1000000),
+        functools.partial(write, parts),
+        out_shape=(shape, shape),
+        in_specs=[inside] * len(held),
+        out_specs=(outside, outside),
+        scratch_shapes=[vmem((2, SUB, rows, cells), f32), dma((4,))],
+        compiler_params=pltpu.CompilerParams(vmem_limit_bytes=3000000),
     )(*kept)
 
 

time: 48.5 us -> 47.6 us (0.981)
  Pallas kernels: 47.7 us -> 46.6 us
    pallas_call x1, Pallas kernels: 45.3 us -> 44.2 us  [shards(): pl.pallas_call(functools.partial(kernel, tiles, levs, groups, rows, modes...]
where the time goes in v5:
time: 47.6 us; the launch traced here: 47.4 us
  Pallas kernels  46.6 us (98%)
  between operations  0.8 us (2%)
    pallas_call x1, Pallas kernels, shards(): pl.pallas_call(functools.partial(kernel, tiles, levs, groups, rows, modes...  44.2 us
    pallas_call x1, Pallas kernels, shards(): pl.pallas_call(functools.partial(write, parts), out_shape=(shape, shape),...  2.37 us

profile of v5, /device:TPU:0, one launch (start us, length us, event | category | flops | bytes accessed | tf_op | source)
XLA Modules:
  0.0 47.4 jit_solution(5921019119505842456)
XLA Ops:
  0.6 44.2 %shard_map.50 = (f32[32,16,1024]{2,1,0:T(8,128)S(1)}, f32[32,16,1024]{2,1,0:T(8,128)S(1)}, f32[5,32,8,1024]{3,2,1,0:T(8,128)S(1)}, f32[184,8,1024]{2,1,0:T(8,128)S(1)}, f32[17,8,128]{2,1,0:T(8,128)S(1)}) custom-call(bf16[1088,1024]{1,0:T(8,128)(2,1)} %bitcast.3, bf16[136,80]{1,0:T(8,128)(2,1)} %bitcast.4, f32[1,40]{1,0:T(1,128)} %bitcast.5), custom_call_target="tpu_custom_call" | custom-call | tf_op jit(solution)/shard_map/pallas_call | solution.py:549
  44.9 2.4 %shard_map.51 = (f32[40,16,1024]{2,1,0:T(8,128)}, f32[40,16,1024]{2,1,0:T(8,128)}) custom-call(f32[32,16,1024]{2,1,0:T(8,128)S(1)} %get-tuple-element.7.sol_in, f32[32,16,1024]{2,1,0:T(8,128)S(1)} %get-tuple-element.8.res_in, f32[5,32,8,1024]{3,2,1,0:T(8,128)S(1)} %get-tuple-element.9.base, f32[184,8,1024]{2,1,0:T(8,128)S(1)} %get-tuple-element.10.tail, ...), custom_call_target="tpu_custom_call" | custom-call | tf_op jit(solution)/shard_map/pallas_call | solution.py:558
